TPU v7x, 32 devices: a whole 2x2x4 slice. The times are simulated.
32 devices in a mesh: grp: 2 (over x), seq: 16 (over z, y, core).
Axes of the slice: x: 2, y: 2, z: 4, core: 2. Of those that a mesh axis runs over, the one named last changes fastest.
Arguments:
- queries: bfloat16 [256, 4096], P(('grp', 'seq')), parts along dimension 0, may hold values from -9 to 9
- question_keys: bfloat16 [256, 2048], P(('grp', 'seq')), parts along dimension 0, may hold values from -4 to 4
- question_values: bfloat16 [256, 2048], P(('grp', 'seq')), parts along dimension 0, may hold values from -5 to 5
- doc_keys: bfloat16 [16384, 2048], P(('grp', 'seq')), parts along dimension 0, may hold values from -4 to 4
- doc_values: bfloat16 [16384, 2048], P(('grp', 'seq')), parts along dimension 0, may hold values from -5 to 5
- lengths: int32 [2], P('grp'), parts along dimension 0, may hold values from 4 to 128
- offsets: int32 [2], P('grp'), parts along dimension 0, may hold values from 2 to 8192, as said below
Outputs:
- attended: bfloat16 [256, 4096], P(('grp', 'seq')), parts along dimension 0
There are 2 independent parts, one for each index of `grp`. A program takes and returns all parts, laid end to end along the dimension named above; each array names one. Nothing has to cross between parts.
Inputs may be any that keep to these rules, and one draw needn't show every extreme that they name: Some question has offsets equal to 8192.
All inputs are finite; a program needn't handle non-finite values.
Results may differ from a plain program's by a relative error of at most 0.0029.
Values may be sent and summed in bfloat16 or wider, within the bound.
A program may use at most 64 MiB of HBM per device.

v0:
```python
import math

import jax
import jax.numpy as jnp
from jax import lax
from jax.sharding import PartitionSpec as P

H = 32
KVH = 16
HD = 128
QSCALE = 144
QL = 128
NQ = 1


MASKED = -1e30


def row_tables(start, count, lengths, offsets):
    rows = start + jnp.arange(count, dtype=jnp.int32)
    question = rows // QL
    position = rows % QL
    owner_table = question[:, None] == jnp.arange(NQ, dtype=jnp.int32)[None, :]
    row_length = jnp.sum(jnp.where(owner_table, lengths[None, :], 0), axis=1)
    row_offset = jnp.sum(jnp.where(owner_table, offsets[None, :], 0), axis=1)
    return (question, position, position < row_length, row_offset)


def local(queries, question_keys, question_values, doc_keys, doc_values, lengths, offsets):
    rows_local = queries.shape[0]
    doc_local = doc_keys.shape[0]
    device_count = lax.axis_size("seq")
    device_index = lax.axis_index("seq")
    total_rows = rows_local * device_count
    per_group = H // KVH
    factor_q = QSCALE ** (-0.5)
    key_doc = doc_keys.reshape(doc_local, KVH, HD)
    value_doc = doc_values.reshape(doc_local, KVH, HD)
    key_self = question_keys.reshape(rows_local, KVH, HD)
    value_self = question_values.reshape(rows_local, KVH, HD)
    doc_places = device_index * doc_local + jnp.arange(doc_local, dtype=jnp.int32)
    self_rows = device_index * rows_local + jnp.arange(rows_local, dtype=jnp.int32)
    whole = lax.all_gather(queries, "seq", axis=0, tiled=True)
    block_rows = math.gcd(total_rows, 512)
    block_count = total_rows // block_rows

    def one_block(start):
        piece = whole.reshape(block_rows, KVH, per_group, HD)
        question, position, live_rows, row_offset = row_tables(start, block_rows, lengths, offsets)
        mask_doc = live_rows[:, None] & (doc_places[None, :] < row_offset[:, None])
        mask_self = (
            live_rows[:, None]
            & (self_rows[None, :] // QL == question[:, None])
            & (self_rows[None, :] % QL <= position[:, None])
        )
        mask_doc = mask_doc[:, None, None, :]
        mask_self = mask_self[:, None, None, :]
        scores_doc = (
            jnp.einsum("rgjd,kgd->rgjk", piece, key_doc, preferred_element_type=jnp.float32)
            * factor_q
        )
        scores_self = (
            jnp.einsum("rgjd,kgd->rgjk", piece, key_self, preferred_element_type=jnp.float32)
            * factor_q
        )
        scores_doc = jnp.where(mask_doc, scores_doc, MASKED)
        scores_self = jnp.where(mask_self, scores_self, MASKED)
        block_top = jnp.maximum(jnp.max(scores_doc, axis=-1), jnp.max(scores_self, axis=-1))
        weights_doc = jnp.where(mask_doc, jnp.exp(scores_doc - block_top[..., None]), 0.0).astype(
            jnp.bfloat16
        )
        weights_self = jnp.where(
            mask_self, jnp.exp(scores_self - block_top[..., None]), 0.0
        ).astype(jnp.bfloat16)
        block_den = jnp.sum(weights_doc.astype(jnp.float32), axis=-1) + jnp.sum(
            weights_self.astype(jnp.float32), axis=-1
        )
        block_num = jnp.einsum(
            "rgjk,kgd->rgjd", weights_doc, value_doc, preferred_element_type=jnp.float32
        )
        block_num = block_num + jnp.einsum(
            "rgjk,kgd->rgjd", weights_self, value_self, preferred_element_type=jnp.float32
        )
        return (
            block_num.reshape(block_rows, H * HD),
            block_top.reshape(block_rows, H),
            block_den.reshape(block_rows, H),
        )

    starts = jnp.arange(block_count, dtype=jnp.int32) * block_rows
    numer, row_top, denom = lax.map(one_block, starts)
    numer = numer.reshape(total_rows, H * HD)
    row_top = row_top.reshape(total_rows, H)
    denom = denom.reshape(total_rows, H)
    got_num, got_top, got_den = (
        lax.all_to_all(numer[None], "seq", split_axis=1, concat_axis=0, tiled=True),
        lax.all_to_all(row_top[None], "seq", split_axis=1, concat_axis=0, tiled=True),
        lax.all_to_all(denom[None], "seq", split_axis=1, concat_axis=0, tiled=True),
    )
    overall = jnp.max(got_top, axis=0)
    rescale = jnp.exp(got_top - overall[None])
    total_num = jnp.sum(
        got_num.reshape(device_count, rows_local, H, HD) * rescale[:, :, :, None], axis=0
    )
    total_den = jnp.sum(got_den * rescale, axis=0)
    question, position, live_rows, row_offset = row_tables(
        device_index * rows_local, rows_local, lengths, offsets
    )
    safe_den = jnp.where(live_rows[:, None], total_den, 1.0)
    result = (total_num / safe_den[:, :, None]).reshape(rows_local, H * HD)
    return jnp.where(live_rows[:, None], result, 0.0).astype(jnp.bfloat16)


def solution(mesh):
    placed = (
        P(("grp", "seq"), None),
        P(("grp", "seq"), None),
        P(("grp", "seq"), None),
        P(("grp", "seq"), None),
        P(("grp", "seq"), None),
        P("grp"),
        P("grp"),
    )
    return jax.shard_map(
        local, mesh=mesh, in_specs=placed, out_specs=P(("grp", "seq"), None), check_vma=False
    )
```

profile of v0, /device:TPU:13, one launch (start us, length us, event | category | flops | bytes accessed | tf_op | source)
XLA Modules:
  0.0 149.6 jit_solution(6486073147577093918)
XLA Ops:
  6.5 0.0 copy-start
  6.5 0.0 copy-start.2
  6.5 0.0 all-gather.2.cloned.1.call-start
  6.5 0.7 all-gather.2.cloned.1.call-update
  8.6 3.6 %copy.52 = bf16[64,8,16,128]{3,2,1,0:T(8,128)(2,1)} copy(bf16[64,8,16,128]{3,1,2,0:T(8,128)(2,1)} %bitcast.72) | data formatting | bytes 4194304
  12.1 0.0 copy-done.2
  12.1 0.0 copy-start.4
  12.1 2.5 %copy.50 = bf16[512,2048]{0,1:T(8,128)(2,1)} copy(bf16[512,2048]{1,0:T(8,128)(2,1)S(1)} %copy-done.2) | data formatting | bytes 4194304 | tf_op jit(solution)/shard_map/reshape | solution.py:38
  14.7 0.1 compare_and_fusion.1
  14.8 0.1 compare_and_fusion
  15.0 32.6 %all-gather.2.cloned.1.call-done = bf16[128,4096]{1,0:T(8,128)(2,1)} async-done(((bf16[8,4096]{1,0:T(8,128)(2,1)}), bf16[128,4096]{1,0:T(8,128)(2,1)}) %all-gather.2.cloned.1.call-update) | async-done | bytes 1048592 | tf_op jit(solution)/shard_map/all_gather | solution.py:43
  47.5 1.6 %copy.30 = bf16[128,4096]{0,1:T(8,128)(2,1)S(1)} copy(bf16[128,4096]{1,0:T(8,128)(2,1)} %all-gather.2.cloned.1.call-done) | data formatting | bytes 2097152 | tf_op jit(solution)/shard_map/all_gather | solution.py:43
  49.2 0.0 copy-done.4
  49.2 0.3 fusion.14
  49.4 3.2 %fusion = (f32[128,16,2]{0,2,1:T(2,128)S(1)}, f32[16,512,128,2]{2,1,3,0:T(8,128)S(1)}) fusion(pred[128,512]{0,1:T(8,128)(4,1)S(1)} %compare_and_fusion, bf16[128,16,2,128]{0,3,2,1:T(8,128)(2,1)S(1)} %bitcast.71, bf16[512,16,128,1]{2,1,0,3:T(8,128)(2,1)} %bitcast.74), kind=kOutput, calls=%fused_computation.3 | convolution fusion | flops 543158272 | bytes 11616256 | tf_op jit(solution)/shard_map/while/body/eval_jaxpr/rgjd,kgd->rgjk/dot_general | solution.py:59
  52.6 0.0 copy-start.1
  52.6 0.0 copy-start.3
  52.7 2.1 %convert_reduce_fusion = f32[128,16,2]{0,2,1:T(2,128)S(1)} fusion(f32[128,16,2]{0,2,1:T(2,128)S(1)} %max.18, f32[16,512,128,2]{2,1,3,0:T(8,128)S(1)} %get-tuple-element.32, pred[128,512]{0,1:T(8,128)(4,1)S(1)} %compare_and_fusion), kind=kLoop, calls=%fused_computation.1 | loop fusion | flops 14675968 | bytes 8486912 | tf_op jit(solution)/shard_map/while/body/eval_jaxpr/reduce_sum | solution.py:75
  54.7 1.4 copy-done.1
  56.2 0.1 convert_reduce_fusion.1
  56.3 0.1 copy.39
  56.4 0.6 broadcast.482
  56.9 0.8 reduce.1
  57.7 0.7 reshape.376
  58.4 5.4 %all-to-all-start.2 = ((f32[16,1,256]{2,1,0:T(1,128)}), f32[16,1,256]{2,1,0:T(1,128)S(1)}, u32[]{:S(2)}, u32[]{:S(2)}) async-start(f32[16,1,256]{2,1,0:T(1,128)} %reshape.376), calls=%async_computation.2 | async-start | bytes 32768 | tf_op jit(solution)/shard_map/all_to_all | solution.py:98
  63.8 0.0 copy-done
  63.8 1.8 %fusion.8 = f32[16,128,2,128]{1,3,2,0:T(8,128)} fusion(bf16[8,2048]{1,0:T(8,128)(2,1)S(1)} %copy-done, f32[128,16,2,8]{0,3,2,1:T(8,128)S(1)} %get-tuple-element.34, f32[128,16,2]{0,2,1:T(2,128)S(1)} %max.18, pred[128,8]{0,1:T(8,128)(4,1)S(1)} %compare_and_fusion.1), kind=kOutput, calls=%fused_computation.20 | convolution fusion | flops 8486912 | bytes 2278400 | tf_op jit(solution)/shard_map/while/body/eval_jaxpr/rgjk,kgd->rgjd/dot_general | solution.py:81
  65.6 0.1 copy.37
  65.7 0.8 reduce.3
  66.5 0.7 reshape.374
  67.2 0.8 all-to-all-done.2
  67.9 5.8 %all-to-all-start.1 = ((f32[16,1,256]{2,1,0:T(1,128)}), f32[16,1,256]{2,1,0:T(1,128)S(1)}, u32[]{:S(2)}, u32[]{:S(2)}) async-start(f32[16,1,256]{2,1,0:T(1,128)} %reshape.374), calls=%async_computation.1 | async-start | bytes 32768 | tf_op jit(solution)/shard_map/all_to_all | solution.py:97
  73.7 0.0 copy-done.3
  73.7 7.3 %convolution_add_fusion = f32[16,128,2,128]{1,3,2,0:T(8,128)} fusion(f32[16,128,2,128]{1,3,2,0:T(8,128)} %fusion.8, bf16[512,16,128,1]{0,2,3,1:T(8,128)(2,1)S(1)} %bitcast.73, f32[16,512,128,2]{2,1,3,0:T(8,128)} %copy-done.1, f32[128,16,2]{0,2,1:T(2,128)S(1)} %max.18, pred[128,512]{0,1:T(8,128)(4,1)S(1)} %compare_and_fusion), kind=kOutput, calls=%fused_computation.8 | convolution fusion | flops 547880960 | bytes 14761984 | tf_op jit(solution)/shard_map/while/body/eval_jaxpr/rgjk,kgd->rgjd/dot_general | solution.py:78
  81.0 5.7 %copy.36 = f32[1,128,4096]{2,0,1:T(1,128)} copy(f32[1,128,4096]{1,2,0:T(8,128)} %bitcast.75) | data formatting | bytes 4194304 | tf_op jit(solution)/shard_map/while/body/jit(dynamic_update_index_in_dim)/broadcast_in_dim | solution.py:91
  86.7 0.0 all-to-all-done.1
  86.7 6.1 %all-to-all-start = ((f32[1,128,4096]{2,0,1:T(1,128)}), f32[1,128,4096]{2,0,1:T(1,128)S(1)}, u32[]{:S(2)}, u32[]{:S(2)}) async-start(f32[1,128,4096]{2,0,1:T(1,128)} %copy.36), calls=%async_computation | async-start | bytes 4194304 | tf_op jit(solution)/shard_map/all_to_all | solution.py:96
  92.8 0.7 reduce.2
  93.4 0.1 reshape.377
  93.6 0.7 reduce.4
  94.2 0.1 reshape.375
  94.4 0.1 copy.38
  94.6 0.1 broadcast_select_fusion
  94.6 0.1 copy.40
  94.7 45.4 %all-to-all-done = f32[1,128,4096]{2,0,1:T(1,128)S(1)} async-done(((f32[1,128,4096]{2,0,1:T(1,128)}), f32[1,128,4096]{2,0,1:T(1,128)S(1)}, u32[]{:S(2)}, u32[]{:S(2)}) %all-to-all-start) | async-done | bytes 2097184 | tf_op jit(solution)/shard_map/all_to_all | solution.py:96
  140.2 1.8 %fusion.1 = f32[8,4096]{1,0:T(8,128)S(1)} fusion(f32[1,128,4096]{2,0,1:T(1,128)S(1)} %all-to-all-done, f32[16,8,32]{1,2,0:T(8,128)S(1)} %copy.38), kind=kLoop, calls=%fused_computation.5 | loop fusion | flops 1015808 | bytes 2244608 | tf_op jit(solution)/shard_map/reduce_sum | solution.py:102
  142.0 0.7 fusion.7
  (10 shorter events, 0.1 us)
Async XLA Ops:
  6.5 57.3 %copy-start = (bf16[8,2048]{1,0:T(8,128)(2,1)S(1)}, bf16[8,2048]{1,0:T(8,128)(2,1)}, u32[]{:S(2)}) copy-start(bf16[8,2048]{1,0:T(8,128)(2,1)} %param.9) | copy-start | bytes 98308
  6.5 5.6 %copy-start.2 = (bf16[512,2048]{1,0:T(8,128)(2,1)S(1)}, bf16[512,2048]{1,0:T(8,128)(2,1)}, u32[]{:S(2)}) copy-start(bf16[512,2048]{1,0:T(8,128)(2,1)} %param.11) | copy-start | bytes 6291460
  6.5 41.0 %all-gather.2.cloned.1.call-start = ((), (), s32[]{:S(2)}) async-start(), calls=%async_computation.3 | async-start | bytes 1114112 | tf_op jit(solution)/shard_map/all_gather | solution.py:43
  12.1 37.0 %copy-start.4 = (bf16[8,2048]{1,0:T(8,128)(2,1)S(1)}, bf16[8,2048]{1,0:T(8,128)(2,1)}, u32[]{:S(2)}) copy-start(bf16[8,2048]{1,0:T(8,128)(2,1)} %param.8) | copy-start | bytes 98308
  52.6 3.6 %copy-start.1 = (f32[16,512,128,2]{2,1,3,0:T(8,128)}, f32[16,512,128,2]{2,1,3,0:T(8,128)S(1)}, u32[]{:S(2)}) copy-start(f32[16,512,128,2]{2,1,3,0:T(8,128)S(1)} %get-tuple-element.32) | copy-start | bytes 25165828
  52.6 21.1 %copy-start.3 = (bf16[512,2048]{0,1:T(8,128)(2,1)S(1)}, bf16[512,2048]{0,1:T(8,128)(2,1)}, u32[]{:S(2)}) copy-start(bf16[512,2048]{0,1:T(8,128)(2,1)} %copy.50) | copy-start | bytes 6291460
  58.4 9.5 %all-to-all-start.2 = ((f32[16,1,256]{2,1,0:T(1,128)}), f32[16,1,256]{2,1,0:T(1,128)S(1)}, u32[]{:S(2)}, u32[]{:S(2)}) async-start(f32[16,1,256]{2,1,0:T(1,128)} %reshape.376), calls=%async_computation.2 | async-start | bytes 32768 | tf_op jit(solution)/shard_map/all_to_all | solution.py:98
  67.9 18.7 %all-to-all-start.1 = ((f32[16,1,256]{2,1,0:T(1,128)}), f32[16,1,256]{2,1,0:T(1,128)S(1)}, u32[]{:S(2)}, u32[]{:S(2)}) async-start(f32[16,1,256]{2,1,0:T(1,128)} %reshape.374), calls=%async_computation.1 | async-start | bytes 32768 | tf_op jit(solution)/shard_map/all_to_all | solution.py:97
  86.7 53.5 %all-to-all-start = ((f32[1,128,4096]{2,0,1:T(1,128)}), f32[1,128,4096]{2,0,1:T(1,128)S(1)}, u32[]{:S(2)}, u32[]{:S(2)}) async-start(f32[1,128,4096]{2,0,1:T(1,128)} %copy.36), calls=%async_computation | async-start | bytes 4194304 | tf_op jit(solution)/shard_map/all_to_all | solution.py:96
Sparse Core Ops, SparseCore 0:
  9.5 38.0 all-gather.1
where the time goes:
time: 150 us
  waiting for transfers between devices  79.5 us (53%)
  local copies, waits for them, and re-layouts  17.5 us (12%)
  starting transfers between devices  17.2 us (11%)
  between operations  14.9 us (10%)
  matrix products  12.5 us (8%)
  other arithmetic  7.99 us (5%)
    all_to_all x1, waiting for transfers between devices, local(): lax.all_to_all(numer[None], 'seq', split_axis=1, concat_axis=0, tiled=True)  45.4 us
    all_gather x1, waiting for transfers between devices, local(): whole = lax.all_gather(queries, 'seq', axis=0, tiled=True)  32.6 us
    dot_general x1, matrix products, one_block(): jnp.einsum('rgjk,kgd->rgjd', weights_doc, value_doc, preferred_element_ty...  7.29 us
    unnamed x16, local copies, waits for them, and re-layouts  7.29 us
    all_to_all x1, starting transfers between devices, local(): lax.all_to_all(numer[None], 'seq', split_axis=1, concat_axis=0, tiled=True)  6.06 us
    all_to_all x1, starting transfers between devices, local(): lax.all_to_all(row_top[None], 'seq', split_axis=1, concat_axis=0, tiled=T...  5.76 us
    broadcast_in_dim x1, local copies, waits for them, and re-layouts, local(): numer, row_top, denom = lax.map(one_block, starts)  5.68 us
    all_to_all x1, starting transfers between devices, local(): lax.all_to_all(denom[None], 'seq', split_axis=1, concat_axis=0, tiled=True)  5.37 us
  transfers between devices with their start and end apart: 4, of which 3 were waited for; matrix products, arithmetic and copies ran while one was open for 16% of the time, Pallas kernels for 0%

commit v1 on v0

--- a/solution.py
+++ b/solution.py
@@ -1,8 +1,11 @@
+import functools
 import math
 
 import jax
 import jax.numpy as jnp
 from jax import lax
+from jax.experimental import pallas as pl
+from jax.experimental.pallas import tpu as pltpu
 from jax.sharding import PartitionSpec as P
 
 H = 32
@@ -111,6 +114,273 @@
     return jnp.where(live_rows[:, None], result, 0.0).astype(jnp.bfloat16)
 
 
+MESH = pl.DeviceIdType.MESH
+LANE = 128
+CHUNKS = 4
+LOG2E = math.log2(math.e)
+WIRE = jnp.int16
+WIRE_TOP = 32767.0
+
+
+def fused_kernel(
+    n, q_ref, qk_ref, qv_ref, k_hbm, v_hbm, len_ref, off_ref, o_ref,
+    kbuf, vbuf, bias, qbuf, nkeep, skeep, nsend, ssend, narr, sarr, wsend, wstat, warr, wsarr,
+    kv_sem, q_send, q_recv, f_send, f_recv, p_send, p_recv, w_send, w_recv,
+):
+    chips = n // 2
+    rows = q_ref.shape[0]
+    doc = k_hbm.shape[0]
+    keys = kbuf.shape[0]
+    half = chips * rows
+    total = 2 * half
+    group_width = (KVH // CHUNKS) * HD
+    wide = (H // CHUNKS) * HD
+    heads = H // CHUNKS
+    per_group = H // KVH
+    me = lax.axis_index("seq")
+    chip, core = me // 2, me % 2
+    partner = chip * 2 + 1 - core
+
+    def peer(d):
+        return lax.rem(chip + d, chips)
+
+    def kv_copies(c):
+        cols = pl.ds(c * group_width, group_width)
+        return (
+            pltpu.make_async_copy(k_hbm.at[:, cols], kbuf.at[pl.ds(0, doc), cols], kv_sem.at[0, c]),
+            pltpu.make_async_copy(v_hbm.at[:, cols], vbuf.at[pl.ds(0, doc), cols], kv_sem.at[1, c]),
+        )
+
+    for c in range(CHUNKS):
+        for copy in kv_copies(c):
+            copy.start()
+    barrier = pltpu.get_barrier_semaphore()
+    for d in range(1, n):
+        pl.semaphore_signal(
+            barrier, inc=1, device_id={"seq": lax.rem(me + d, n)}, device_id_type=MESH
+        )
+
+    for buf, own in ((kbuf, qk_ref), (vbuf, qv_ref)):
+        wide_own = own[...].astype(jnp.float32)
+        pad = jnp.zeros((keys - doc - rows, own.shape[1]), jnp.float32)
+        buf[doc:, :] = jnp.concatenate([wide_own, pad], axis=0).astype(buf.dtype)
+    for c in range(CHUNKS):
+        qbuf[c, 0, chip] = q_ref[:, c * wide : (c + 1) * wide]
+    slot = lax.broadcasted_iota(jnp.int32, (total, keys), 0)
+    place = lax.broadcasted_iota(jnp.int32, (total, keys), 1)
+    side = slot // half
+    inner = slot % half
+    row = (2 * (inner // rows) + jnp.where(side == 0, core, 1 - core)) * rows + inner % rows
+    question, position = row // QL, row % QL
+    row_length = jnp.zeros_like(row)
+    row_offset = jnp.zeros_like(row)
+    for i in range(NQ):
+        row_length = jnp.where(question == i, len_ref[i], row_length)
+        row_offset = jnp.where(question == i, off_ref[i], row_offset)
+    self_row = me * rows + place - doc
+    seen_doc = (place < doc) & (me * doc + place < row_offset)
+    seen_self = (
+        (place >= doc) & (place < doc + rows)
+        & (self_row // QL == question) & (self_row % QL <= position)
+    )
+    bias[...] = jnp.where((position < row_length) & (seen_doc | seen_self), 0.0, MASKED)
+    pl.semaphore_wait(barrier, n - 1)
+
+    def q_copy(c, d):
+        return pltpu.make_async_remote_copy(
+            q_ref.at[:, pl.ds(c * wide, wide)], qbuf.at[c, 0, chip],
+            q_send.at[c, d], q_recv.at[c, d],
+            device_id={"seq": peer(d) * 2 + core}, device_id_type=MESH,
+        )
+
+    def f_copy(c, d):
+        source = q_ref.at[:, pl.ds(c * wide, wide)] if d == 0 else qbuf.at[c, 0, peer(chips - d)]
+        return pltpu.make_async_remote_copy(
+            source, qbuf.at[c, 1, peer(chips - d)], f_send.at[c, d], f_recv.at[c, d],
+            device_id={"seq": partner}, device_id_type=MESH,
+        )
+
+    def p_copies(c):
+        return tuple(
+            pltpu.make_async_remote_copy(
+                a.at[c], b.at[c], p_send.at[c, i], p_recv.at[c, i],
+                device_id={"seq": partner}, device_id_type=MESH,
+            )
+            for i, (a, b) in enumerate(((nsend, narr), (ssend, sarr)))
+        )
+
+    def w_copies(c, d):
+        return tuple(
+            pltpu.make_async_remote_copy(
+                a.at[c, peer(d)], b.at[c, chip], w_send.at[c, i, d], w_recv.at[c, i, d],
+                device_id={"seq": peer(d) * 2 + core}, device_id_type=MESH,
+            )
+            for i, (a, b) in enumerate(((wsend, warr), (wstat, wsarr)))
+        )
+
+    for c in range(CHUNKS):
+        f_copy(c, 0).start()
+        for d in range(1, chips):
+            q_copy(c, d).start()
+
+    factor = QSCALE ** (-0.5) * LOG2E
+
+    def attend(c):
+        for g in range(KVH // CHUNKS):
+            cols = slice(c * group_width + g * HD, c * group_width + (g + 1) * HD)
+            key, value = kbuf[:, cols], vbuf[:, cols]
+            pieces = []
+            for j in range(per_group):
+                h = g * per_group + j
+                block = qbuf[c, :, :, :, h * HD : (h + 1) * HD].astype(jnp.float32)
+                pieces.append(block.reshape(total, HD).astype(jnp.bfloat16))
+            query = jnp.concatenate(pieces, axis=0)
+            scores = lax.dot_general(
+                query, key, (((1,), (1,)), ((), ())), preferred_element_type=jnp.float32
+            )
+            for j in range(per_group):
+                h = g * per_group + j
+                part = scores[j * total : (j + 1) * total] * factor + bias[...]
+                top = jnp.max(part, axis=1, keepdims=True)
+                weights = jnp.exp2(part - top).astype(jnp.bfloat16)
+                den = jnp.sum(weights.astype(jnp.float32), axis=1, keepdims=True)
+                num = jnp.dot(weights, value, preferred_element_type=jnp.float32)
+                hc = slice(h * HD, (h + 1) * HD)
+                nkeep[c, :, hc] = num[:half]
+                nsend[c, :, hc] = num[half:]
+                for stat, buf in ((top, 0), (den, heads)):
+                    skeep[c, :, buf + h : buf + h + 1] = stat[:half]
+                    ssend[c, :, buf + h : buf + h + 1] = stat[half:]
+
+    def pair_up(c):
+        for copy in p_copies(c):
+            copy.wait_recv()
+        stat_a, stat_b = skeep[c], sarr[c]
+        top_a, top_b = stat_a[:, :heads], stat_b[:, :heads]
+        top = jnp.maximum(top_a, top_b)
+        fa, fb = jnp.exp2(top_a - top), jnp.exp2(top_b - top)
+        den = stat_a[:, heads : 2 * heads] * fa + stat_b[:, heads : 2 * heads] * fb
+        for h in range(heads):
+            hc = slice(h * HD, (h + 1) * HD)
+            num = nkeep[c, :, hc] * fa[:, h : h + 1] + narr[c, :, hc] * fb[:, h : h + 1]
+            largest = jnp.maximum(jnp.max(jnp.abs(num), axis=1, keepdims=True), 1e-30)
+            wsend[c, :, :, hc] = encode(num / largest).reshape(chips, rows, HD)
+            for stat, at in ((top[:, h : h + 1], h), (den[:, h : h + 1], heads + h), (largest, 2 * heads + h)):
+                wstat[c, :, :, at : at + 1] = stat.reshape(chips, rows, 1)
+        for d in range(1, chips):
+            for copy in w_copies(c, d):
+                copy.start()
+        warr[c, chip] = wsend[c, chip]
+        wsarr[c, chip] = wstat[c, chip]
+
+    for c in range(CHUNKS):
+        for d in range(1, chips):
+            q_copy(c, d).wait_recv()
+            f_copy(c, d).start()
+        for d in range(chips):
+            f_copy(c, d).wait_recv()
+        for copy in kv_copies(c):
+            copy.wait()
+        attend(c)
+        for copy in p_copies(c):
+            copy.start()
+        if c > 0:
+            pair_up(c - 1)
+    pair_up(CHUNKS - 1)
+
+    mine = me * rows + lax.broadcasted_iota(jnp.int32, (rows, HD), 0)
+    live_to = jnp.zeros_like(mine)
+    for i in range(NQ):
+        live_to = jnp.where(mine // QL == i, len_ref[i], live_to)
+    live = mine % QL < live_to
+    for c in range(CHUNKS):
+        for d in range(1, chips):
+            for copy in w_copies(c, d):
+                copy.wait_recv()
+        tops = [wsarr[c, k][:, :heads] for k in range(chips)]
+        overall = functools.reduce(jnp.maximum, tops)
+        shrink = [jnp.exp2(t - overall) for t in tops]
+        den = sum(wsarr[c, k][:, heads : 2 * heads] * shrink[k] for k in range(chips))
+        coefs = [wsarr[c, k][:, 2 * heads : 3 * heads] * shrink[k] / den for k in range(chips)]
+        for h in range(heads):
+            hc = slice(h * HD, (h + 1) * HD)
+            acc = jnp.zeros((rows, HD), jnp.float32)
+            for k in range(chips):
+                acc = acc + decode(warr[c, k, :, hc]) * coefs[k][:, h : h + 1]
+            o_ref[:, c * wide + h * HD : c * wide + (h + 1) * HD] = jnp.where(live, acc, 0.0).astype(
+                o_ref.dtype
+            )
+    for c in range(CHUNKS):
+        f_copy(c, 0).wait_send()
+        for d in range(1, chips):
+            q_copy(c, d).wait_send()
+            f_copy(c, d).wait_send()
+            for copy in w_copies(c, d):
+                copy.wait_send()
+        for copy in p_copies(c):
+            copy.wait_send()
+
+
+def encode(x):
+    return jnp.round(x * WIRE_TOP).astype(jnp.int32).astype(WIRE)
+
+
+def decode(x):
+    return x.astype(jnp.int32).astype(jnp.float32) * (1.0 / WIRE_TOP)
+
+
+def fused(n, queries, question_keys, question_values, doc_keys, doc_values, lengths, offsets):
+    rows = queries.shape[0]
+    doc = doc_keys.shape[0]
+    if rows % 8 or n % 2 or n * rows > 256 or doc % LANE or doc > 1024:
+        return local(
+            queries, question_keys, question_values, doc_keys, doc_values, lengths, offsets
+        )
+    chips = n // 2
+    half = chips * rows
+    keys = doc + -(-rows // LANE) * LANE
+    wide = H * HD // CHUNKS
+    vmem = pl.BlockSpec(memory_space=pltpu.VMEM)
+    smem = pl.BlockSpec(memory_space=pltpu.SMEM)
+    hbm = pl.BlockSpec(memory_space=pl.ANY)
+    f32 = jnp.float32
+    dma = pltpu.SemaphoreType.DMA
+    return pl.pallas_call(
+        functools.partial(fused_kernel, n),
+        out_shape=jax.ShapeDtypeStruct(queries.shape, jnp.bfloat16),
+        in_specs=[vmem, vmem, vmem, hbm, hbm, smem, smem],
+        out_specs=vmem,
+        scratch_shapes=[
+            pltpu.VMEM((keys, KVH * HD), jnp.bfloat16),
+            pltpu.VMEM((keys, KVH * HD), jnp.bfloat16),
+            pltpu.VMEM((2 * half, keys), f32),
+            pltpu.VMEM((CHUNKS, 2, chips, rows, wide), jnp.bfloat16),
+            pltpu.VMEM((CHUNKS, half, wide), f32),
+            pltpu.VMEM((CHUNKS, half, LANE), f32),
+            pltpu.VMEM((CHUNKS, half, wide), f32),
+            pltpu.VMEM((CHUNKS, half, LANE), f32),
+            pltpu.VMEM((CHUNKS, half, wide), f32),
+            pltpu.VMEM((CHUNKS, half, LANE), f32),
+            pltpu.VMEM((CHUNKS, chips, rows, wide), WIRE),
+            pltpu.VMEM((CHUNKS, chips, rows, LANE), f32),
+            pltpu.VMEM((CHUNKS, chips, rows, wide), WIRE),
+            pltpu.VMEM((CHUNKS, chips, rows, LANE), f32),
+            dma((2, CHUNKS)),
+            dma((CHUNKS, chips)),
+            dma((CHUNKS, chips)),
+            dma((CHUNKS, chips)),
+            dma((CHUNKS, chips)),
+            dma((CHUNKS, 2)),
+            dma((CHUNKS, 2)),
+            dma((CHUNKS, 2, chips)),
+            dma((CHUNKS, 2, chips)),
+        ],
+        compiler_params=pltpu.CompilerParams(
+            collective_id=0, has_side_effects=True, vmem_limit_bytes=60 * 1024 * 1024
+        ),
+    )(queries, question_keys, question_values, doc_keys, doc_values, lengths, offsets)
+
+
 def solution(mesh):
     placed = (
         P(("grp", "seq"), None),
@@ -122,5 +392,6 @@
         P("grp"),
     )
     return jax.shard_map(
-        local, mesh=mesh, in_specs=placed, out_specs=P(("grp", "seq"), None), check_vma=False
-    )
+        functools.partial(fused, mesh.shape["seq"]),
+        mesh=mesh, in_specs=placed, out_specs=P(("grp", "seq"), None), check_vma=False,
+    )

time: 150 us -> 41.4 us (0.28)
  the two profiles are of different devices: /device:TPU:13 before, /device:TPU:0 now
where the time goes in v1:
time: 41.4 us; the launch traced here: 40.6 us
  Pallas kernels  37.8 us (91%)
  local copies, waits for them, and re-layouts  1.47 us (4%)
  between operations  1.3 us (3%)
    pallas_call x1, Pallas kernels, fused(): pl.pallas_call(functools.partial(fused_kernel, n), out_shape=jax.ShapeDty...  37.8 us
    unnamed x1, local copies, waits for them, and re-layouts  1.47 us

profile of v1, /device:TPU:0, one launch (start us, length us, event | category | flops | bytes accessed | tf_op | source)
XLA Modules:
  0.0 40.6 jit_solution(443971422403472222)
XLA Ops:
  1.3 37.8 %shard_map.73 = bf16[8,4096]{1,0:T(8,128)(2,1)} custom-call(bf16[8,4096]{1,0:T(8,128)(2,1)} %q_ref.1, bf16[8,2048]{1,0:T(8,128)(2,1)} %qk_ref.1, bf16[8,2048]{1,0:T(8,128)(2,1)} %qv_ref.1, bf16[512,2048]{1,0:T(8,128)(2,1)} %k_hbm.1, bf16[512,2048]{1,0:T(8,128)(2,1)} %v_hbm.1, s32[1]{0:T(128)S(6)} %copy.9.len_ref, s32[1]{0:T(128)S(6)} %copy.10.off_ref), custom_call_target="tpu_custom_call" | custom-call | tf_op jit(solution)/shard_map/pallas_call | solution.py:348
  39.1 1.5 %copy.11 = bf16[8,4096]{1,0:T(8,128)(2,1)} copy(bf16[8,4096]{1,0:T(8,128)(2,1)} %shard_map.73) | data formatting | bytes 131072

commit v2 on v1

--- a/solution.py
+++ b/solution.py
@@ -125,7 +125,7 @@
 def fused_kernel(
     n, q_ref, qk_ref, qv_ref, k_hbm, v_hbm, len_ref, off_ref, o_ref,
     kbuf, vbuf, bias, qbuf, nkeep, skeep, nsend, ssend, narr, sarr, wsend, wstat, warr, wsarr,
-    kv_sem, q_send, q_recv, f_send, f_recv, p_send, p_recv, w_send, w_recv,
+    kv_sem, q_send, q_recv, t_send, t_recv, f_send, f_recv, p_send, p_recv, w_send, w_recv,
 ):
     chips = n // 2
     rows = q_ref.shape[0]
@@ -166,8 +166,8 @@
         buf[doc:, :] = jnp.concatenate([wide_own, pad], axis=0).astype(buf.dtype)
     for c in range(CHUNKS):
         qbuf[c, 0, chip] = q_ref[:, c * wide : (c + 1) * wide]
-    slot = lax.broadcasted_iota(jnp.int32, (total, keys), 0)
-    place = lax.broadcasted_iota(jnp.int32, (total, keys), 1)
+    slot = lax.broadcasted_iota(jnp.int32, (total, 1), 0)
+    place = lax.broadcasted_iota(jnp.int32, (1, keys), 1)
     side = slot // half
     inner = slot % half
     row = (2 * (inner // rows) + jnp.where(side == 0, core, 1 - core)) * rows + inner % rows
@@ -177,26 +177,45 @@
     for i in range(NQ):
         row_length = jnp.where(question == i, len_ref[i], row_length)
         row_offset = jnp.where(question == i, off_ref[i], row_offset)
-    self_row = me * rows + place - doc
-    seen_doc = (place < doc) & (me * doc + place < row_offset)
+    doc_end = jnp.where(position < row_length, row_offset - me * doc, 0)
+    self_end = jnp.where(position < row_length, row + 1 - me * rows + doc, 0)
+    self_start = question * QL - me * rows + doc
+    wide_place = jnp.broadcast_to(place, (total, keys))
+    seen_doc = (wide_place < doc) & (wide_place < doc_end)
     seen_self = (
-        (place >= doc) & (place < doc + rows)
-        & (self_row // QL == question) & (self_row % QL <= position)
-    )
-    bias[...] = jnp.where((position < row_length) & (seen_doc | seen_self), 0.0, MASKED)
+        (wide_place >= doc) & (wide_place < doc + rows)
+        & (wide_place >= self_start) & (wide_place < self_end)
+    )
+    bias[...] = jnp.where(seen_doc | seen_self, 0.0, MASKED)
     pl.semaphore_wait(barrier, n - 1)
 
+    lines = chips // 2
+    line, col = chip // 2, chip % 2
+
+    def source_chip(e, d):
+        return lax.rem(line + lines - d, lines) * 2 + (col if e == 0 else 1 - col)
+
+    def held(c, e, d):
+        own = e == 0 and d == 0
+        return q_ref.at[:, pl.ds(c * wide, wide)] if own else qbuf.at[c, 0, source_chip(e, d)]
+
     def q_copy(c, d):
+        target = lax.rem(line + d, lines) * 2 + col
         return pltpu.make_async_remote_copy(
-            q_ref.at[:, pl.ds(c * wide, wide)], qbuf.at[c, 0, chip],
-            q_send.at[c, d], q_recv.at[c, d],
-            device_id={"seq": peer(d) * 2 + core}, device_id_type=MESH,
-        )
-
-    def f_copy(c, d):
-        source = q_ref.at[:, pl.ds(c * wide, wide)] if d == 0 else qbuf.at[c, 0, peer(chips - d)]
+            held(c, 0, 0), qbuf.at[c, 0, chip], q_send.at[c, d], q_recv.at[c, d],
+            device_id={"seq": target * 2 + core}, device_id_type=MESH,
+        )
+
+    def t_copy(c, d):
         return pltpu.make_async_remote_copy(
-            source, qbuf.at[c, 1, peer(chips - d)], f_send.at[c, d], f_recv.at[c, d],
+            held(c, 0, d), qbuf.at[c, 0, source_chip(0, d)], t_send.at[c, d], t_recv.at[c, d],
+            device_id={"seq": (line * 2 + 1 - col) * 2 + core}, device_id_type=MESH,
+        )
+
+    def f_copy(c, e, d):
+        return pltpu.make_async_remote_copy(
+            held(c, e, d), qbuf.at[c, 1, source_chip(e, d)],
+            f_send.at[c, e, d], f_recv.at[c, e, d],
             device_id={"seq": partner}, device_id_type=MESH,
         )
 
@@ -219,9 +238,10 @@
         )
 
     for c in range(CHUNKS):
-        f_copy(c, 0).start()
-        for d in range(1, chips):
+        for d in range(1, lines):
             q_copy(c, d).start()
+        t_copy(c, 0).start()
+        f_copy(c, 0, 0).start()
 
     factor = QSCALE ** (-0.5) * LOG2E
 
@@ -247,8 +267,9 @@
                 num = jnp.dot(weights, value, preferred_element_type=jnp.float32)
                 hc = slice(h * HD, (h + 1) * HD)
                 nkeep[c, :, hc] = num[:half]
-                nsend[c, :, hc] = num[half:]
-                for stat, buf in ((top, 0), (den, heads)):
+                largest = row_scale(num)
+                nsend[c, :, hc] = encode(num[half:] * (WIRE_TOP / largest[half:]))
+                for stat, buf in ((top, 0), (den, heads), (largest, 2 * heads)):
                     skeep[c, :, buf + h : buf + h + 1] = stat[:half]
                     ssend[c, :, buf + h : buf + h + 1] = stat[half:]
 
@@ -259,12 +280,13 @@
         top_a, top_b = stat_a[:, :heads], stat_b[:, :heads]
         top = jnp.maximum(top_a, top_b)
         fa, fb = jnp.exp2(top_a - top), jnp.exp2(top_b - top)
+        fc = fb * stat_b[:, 2 * heads : 3 * heads]
         den = stat_a[:, heads : 2 * heads] * fa + stat_b[:, heads : 2 * heads] * fb
         for h in range(heads):
             hc = slice(h * HD, (h + 1) * HD)
-            num = nkeep[c, :, hc] * fa[:, h : h + 1] + narr[c, :, hc] * fb[:, h : h + 1]
-            largest = jnp.maximum(jnp.max(jnp.abs(num), axis=1, keepdims=True), 1e-30)
-            wsend[c, :, :, hc] = encode(num / largest).reshape(chips, rows, HD)
+            num = nkeep[c, :, hc] * fa[:, h : h + 1] + decode(narr[c, :, hc]) * fc[:, h : h + 1]
+            largest = row_scale(num)
+            wsend[c, :, :, hc] = encode(num * (WIRE_TOP / largest)).reshape(chips, rows, HD)
             for stat, at in ((top[:, h : h + 1], h), (den[:, h : h + 1], heads + h), (largest, 2 * heads + h)):
                 wstat[c, :, :, at : at + 1] = stat.reshape(chips, rows, 1)
         for d in range(1, chips):
@@ -273,12 +295,28 @@
         warr[c, chip] = wsend[c, chip]
         wsarr[c, chip] = wstat[c, chip]
 
-    for c in range(CHUNKS):
-        for d in range(1, chips):
-            q_copy(c, d).wait_recv()
-            f_copy(c, d).start()
-        for d in range(chips):
-            f_copy(c, d).wait_recv()
+    def relay_line(c):
+        if c < CHUNKS:
+            for d in range(1, lines):
+                q_copy(c, d).wait_recv()
+                t_copy(c, d).start()
+                f_copy(c, 0, d).start()
+
+    def relay_twin(c):
+        if c < CHUNKS:
+            for d in range(lines):
+                t_copy(c, d).wait_recv()
+                f_copy(c, 1, d).start()
+
+    relay_line(0)
+    relay_line(1)
+    relay_twin(0)
+    for c in range(CHUNKS):
+        relay_line(c + 2)
+        relay_twin(c + 1)
+        for e in range(2):
+            for d in range(lines):
+                f_copy(c, e, d).wait_recv()
         for copy in kv_copies(c):
             copy.wait()
         attend(c)
@@ -311,18 +349,25 @@
                 o_ref.dtype
             )
     for c in range(CHUNKS):
-        f_copy(c, 0).wait_send()
+        for d in range(1, lines):
+            q_copy(c, d).wait_send()
+        for d in range(lines):
+            t_copy(c, d).wait_send()
+            for e in range(2):
+                f_copy(c, e, d).wait_send()
         for d in range(1, chips):
-            q_copy(c, d).wait_send()
-            f_copy(c, d).wait_send()
             for copy in w_copies(c, d):
                 copy.wait_send()
         for copy in p_copies(c):
             copy.wait_send()
 
 
+def row_scale(x):
+    return jnp.maximum(jnp.max(jnp.abs(x), axis=1, keepdims=True), 1e-30)
+
+
 def encode(x):
-    return jnp.round(x * WIRE_TOP).astype(jnp.int32).astype(WIRE)
+    return jnp.round(x).astype(jnp.int32).astype(WIRE)
 
 
 def decode(x):
@@ -332,7 +377,7 @@
 def fused(n, queries, question_keys, question_values, doc_keys, doc_values, lengths, offsets):
     rows = queries.shape[0]
     doc = doc_keys.shape[0]
-    if rows % 8 or n % 2 or n * rows > 256 or doc % LANE or doc > 1024:
+    if rows % 8 or n % 4 or n * rows > 256 or doc % LANE or doc > 1024:
         return local(
             queries, question_keys, question_values, doc_keys, doc_values, lengths, offsets
         )
@@ -357,19 +402,21 @@
             pltpu.VMEM((CHUNKS, 2, chips, rows, wide), jnp.bfloat16),
             pltpu.VMEM((CHUNKS, half, wide), f32),
             pltpu.VMEM((CHUNKS, half, LANE), f32),
-            pltpu.VMEM((CHUNKS, half, wide), f32),
+            pltpu.VMEM((CHUNKS, half, wide), WIRE),
             pltpu.VMEM((CHUNKS, half, LANE), f32),
-            pltpu.VMEM((CHUNKS, half, wide), f32),
+            pltpu.VMEM((CHUNKS, half, wide), WIRE),
             pltpu.VMEM((CHUNKS, half, LANE), f32),
             pltpu.VMEM((CHUNKS, chips, rows, wide), WIRE),
             pltpu.VMEM((CHUNKS, chips, rows, LANE), f32),
             pltpu.VMEM((CHUNKS, chips, rows, wide), WIRE),
             pltpu.VMEM((CHUNKS, chips, rows, LANE), f32),
             dma((2, CHUNKS)),
-            dma((CHUNKS, chips)),
-            dma((CHUNKS, chips)),
-            dma((CHUNKS, chips)),
-            dma((CHUNKS, chips)),
+            dma((CHUNKS, chips // 2)),
+            dma((CHUNKS, chips // 2)),
+            dma((CHUNKS, chips // 2)),
+            dma((CHUNKS, chips // 2)),
+            dma((CHUNKS, 2, chips // 2)),
+            dma((CHUNKS, 2, chips // 2)),
             dma((CHUNKS, 2)),
             dma((CHUNKS, 2)),
             dma((CHUNKS, 2, chips)),

time: 41.4 us -> 42 us (1.014); the launches traced: 40.6 us -> 41.8 us
  Pallas kernels: 37.8 us -> 39 us
    pallas_call x1, Pallas kernels: 37.8 us -> 39 us  [fused(): pl.pallas_call(functools.partial(fused_kernel, n), out_shape=jax.ShapeDty...]
where the time goes in v2:
time: 42 us; the launch traced here: 41.8 us
  Pallas kernels  39 us (93%)
  local copies, waits for them, and re-layouts  1.47 us (4%)
  between operations  1.3 us (3%)
    pallas_call x1, Pallas kernels, fused(): pl.pallas_call(functools.partial(fused_kernel, n), out_shape=jax.ShapeDty...  39 us
    unnamed x1, local copies, waits for them, and re-layouts  1.47 us

profile of v2, /device:TPU:0, one launch (start us, length us, event | category | flops | bytes accessed | tf_op | source)
XLA Modules:
  0.0 41.8 jit_solution(9749825587096638536)
XLA Ops:
  1.3 39.0 %shard_map.73 = bf16[8,4096]{1,0:T(8,128)(2,1)} custom-call(bf16[8,4096]{1,0:T(8,128)(2,1)} %q_ref.1, bf16[8,2048]{1,0:T(8,128)(2,1)} %qk_ref.1, bf16[8,2048]{1,0:T(8,128)(2,1)} %qv_ref.1, bf16[512,2048]{1,0:T(8,128)(2,1)} %k_hbm.1, bf16[512,2048]{1,0:T(8,128)(2,1)} %v_hbm.1, s32[1]{0:T(128)S(6)} %copy.9.len_ref, s32[1]{0:T(128)S(6)} %copy.10.off_ref), custom_call_target="tpu_custom_call" | custom-call | tf_op jit(solution)/shard_map/pallas_call | solution.py:393
  40.3 1.5 %copy.11 = bf16[8,4096]{1,0:T(8,128)(2,1)} copy(bf16[8,4096]{1,0:T(8,128)(2,1)} %shard_map.73) | data formatting | bytes 131072

commit v3 on v1

--- a/solution.py
+++ b/solution.py
@@ -209,13 +209,16 @@
             for i, (a, b) in enumerate(((nsend, narr), (ssend, sarr)))
         )
 
-    def w_copies(c, d):
-        return tuple(
-            pltpu.make_async_remote_copy(
-                a.at[c, peer(d)], b.at[c, chip], w_send.at[c, i, d], w_recv.at[c, i, d],
-                device_id={"seq": peer(d) * 2 + core}, device_id_type=MESH,
-            )
-            for i, (a, b) in enumerate(((wsend, warr), (wstat, wsarr)))
+    def w_copy(c, d):
+        return pltpu.make_async_remote_copy(
+            wsend.at[c, peer(d)], warr.at[c, chip], w_send.at[c, d], w_recv.at[c, d],
+            device_id={"seq": peer(d) * 2 + core}, device_id_type=MESH,
+        )
+
+    def s_copy(d):
+        return pltpu.make_async_remote_copy(
+            wstat.at[peer(d)], wsarr.at[chip], w_send.at[CHUNKS, d], w_recv.at[CHUNKS, d],
+            device_id={"seq": peer(d) * 2 + core}, device_id_type=MESH,
         )
 
     for c in range(CHUNKS):
@@ -265,13 +268,16 @@
             num = nkeep[c, :, hc] * fa[:, h : h + 1] + narr[c, :, hc] * fb[:, h : h + 1]
             largest = jnp.maximum(jnp.max(jnp.abs(num), axis=1, keepdims=True), 1e-30)
             wsend[c, :, :, hc] = encode(num / largest).reshape(chips, rows, HD)
-            for stat, at in ((top[:, h : h + 1], h), (den[:, h : h + 1], heads + h), (largest, 2 * heads + h)):
-                wstat[c, :, :, at : at + 1] = stat.reshape(chips, rows, 1)
+            for kind, stat in enumerate((top[:, h : h + 1], den[:, h : h + 1], largest)):
+                at = (c * 3 + kind) * heads + h
+                wstat[:, :, at : at + 1] = stat.reshape(chips, rows, 1)
         for d in range(1, chips):
-            for copy in w_copies(c, d):
-                copy.start()
+            if c == CHUNKS - 1:
+                s_copy(d).start()
+            w_copy(c, d).start()
         warr[c, chip] = wsend[c, chip]
-        wsarr[c, chip] = wstat[c, chip]
+        if c == CHUNKS - 1:
+            wsarr[chip] = wstat[chip]
 
     for c in range(CHUNKS):
         for d in range(1, chips):
@@ -293,15 +299,17 @@
     for i in range(NQ):
         live_to = jnp.where(mine // QL == i, len_ref[i], live_to)
     live = mine % QL < live_to
+    for d in range(1, chips):
+        s_copy(d).wait_recv()
     for c in range(CHUNKS):
         for d in range(1, chips):
-            for copy in w_copies(c, d):
-                copy.wait_recv()
-        tops = [wsarr[c, k][:, :heads] for k in range(chips)]
+            w_copy(c, d).wait_recv()
+        top_at, den_at, scale_at = ((c * 3 + kind) * heads for kind in range(3))
+        tops = [wsarr[k][:, top_at : top_at + heads] for k in range(chips)]
         overall = functools.reduce(jnp.maximum, tops)
         shrink = [jnp.exp2(t - overall) for t in tops]
-        den = sum(wsarr[c, k][:, heads : 2 * heads] * shrink[k] for k in range(chips))
-        coefs = [wsarr[c, k][:, 2 * heads : 3 * heads] * shrink[k] / den for k in range(chips)]
+        den = sum(wsarr[k][:, den_at : den_at + heads] * shrink[k] for k in range(chips))
+        coefs = [wsarr[k][:, scale_at : scale_at + heads] * shrink[k] / den for k in range(chips)]
         for h in range(heads):
             hc = slice(h * HD, (h + 1) * HD)
             acc = jnp.zeros((rows, HD), jnp.float32)
@@ -315,10 +323,11 @@
         for d in range(1, chips):
             q_copy(c, d).wait_send()
             f_copy(c, d).wait_send()
-            for copy in w_copies(c, d):
-                copy.wait_send()
+            w_copy(c, d).wait_send()
         for copy in p_copies(c):
             copy.wait_send()
+    for d in range(1, chips):
+        s_copy(d).wait_send()
 
 
 def encode(x):
@@ -332,7 +341,7 @@
 def fused(n, queries, question_keys, question_values, doc_keys, doc_values, lengths, offsets):
     rows = queries.shape[0]
     doc = doc_keys.shape[0]
-    if rows % 8 or n % 2 or n * rows > 256 or doc % LANE or doc > 1024:
+    if rows % 8 or n % 2 or n * rows > 256 or doc % LANE or doc > 1024 or 3 * H > LANE:
         return local(
             queries, question_keys, question_values, doc_keys, doc_values, lengths, offsets
         )
@@ -362,9 +371,9 @@
             pltpu.VMEM((CHUNKS, half, wide), f32),
             pltpu.VMEM((CHUNKS, half, LANE), f32),
             pltpu.VMEM((CHUNKS, chips, rows, wide), WIRE),
-            pltpu.VMEM((CHUNKS, chips, rows, LANE), f32),
+            pltpu.VMEM((chips, rows, LANE), f32),
             pltpu.VMEM((CHUNKS, chips, rows, wide), WIRE),
-            pltpu.VMEM((CHUNKS, chips, rows, LANE), f32),
+            pltpu.VMEM((chips, rows, LANE), f32),
             dma((2, CHUNKS)),
             dma((CHUNKS, chips)),
             dma((CHUNKS, chips)),
@@ -372,8 +381,8 @@
             dma((CHUNKS, chips)),
             dma((CHUNKS, 2)),
             dma((CHUNKS, 2)),
-            dma((CHUNKS, 2, chips)),
-            dma((CHUNKS, 2, chips)),
+            dma((CHUNKS + 1, chips)),
+            dma((CHUNKS + 1, chips)),
         ],
         compiler_params=pltpu.CompilerParams(
             collective_id=0, has_side_effects=True, vmem_limit_bytes=60 * 1024 * 1024

time: 41.4 us -> 41.1 us (level); the launches traced: 40.6 us -> 40.8 us
  no operation moved by 1% of the time
where the time goes in v3:
time: 41.1 us; the launch traced here: 40.8 us
  Pallas kernels  38.1 us (93%)
  local copies, waits for them, and re-layouts  1.47 us (4%)
  between operations  1.3 us (3%)
    pallas_call x1, Pallas kernels, fused(): pl.pallas_call(functools.partial(fused_kernel, n), out_shape=jax.ShapeDty...  38.1 us
    unnamed x1, local copies, waits for them, and re-layouts  1.47 us

profile of v3, /device:TPU:0, one launch (start us, length us, event | category | flops | bytes accessed | tf_op | source)
XLA Modules:
  0.0 40.8 jit_solution(8188790791552631396)
XLA Ops:
  1.3 38.1 %shard_map.73 = bf16[8,4096]{1,0:T(8,128)(2,1)} custom-call(bf16[8,4096]{1,0:T(8,128)(2,1)} %q_ref.1, bf16[8,2048]{1,0:T(8,128)(2,1)} %qk_ref.1, bf16[8,2048]{1,0:T(8,128)(2,1)} %qv_ref.1, bf16[512,2048]{1,0:T(8,128)(2,1)} %k_hbm.1, bf16[512,2048]{1,0:T(8,128)(2,1)} %v_hbm.1, s32[1]{0:T(128)S(6)} %copy.9.len_ref, s32[1]{0:T(128)S(6)} %copy.10.off_ref), custom_call_target="tpu_custom_call" | custom-call | tf_op jit(solution)/shard_map/pallas_call | solution.py:357
  39.4 1.5 %copy.11 = bf16[8,4096]{1,0:T(8,128)(2,1)} copy(bf16[8,4096]{1,0:T(8,128)(2,1)} %shard_map.73) | data formatting | bytes 131072
